TPU v7x, 32 devices: a whole 2x2x4 slice. The times are simulated.
32 devices in a mesh: lat: 8 (over y, x, core), lon: 4 (over z).
Axes of the slice: x: 2, y: 2, z: 4, core: 2. Of those that a mesh axis runs over, the one named last changes fastest.
Arguments:
- loadings: float32 [176, 720, 200], P('lat', 'lon'), may hold values from -60 to 60, as said below
Outputs:
- rotated: float32 [176, 720, 200], P('lat', 'lon')
- rotation: float32 [200, 200], replicated
Inputs may be any that keep to these rules, and one draw needn't show every extreme that they name: Every grid point's loadings are not all zero.
All inputs are finite; a program needn't handle non-finite values.
Results may differ from a plain program's by a relative error of at most 0.00011.
Values sent between devices are 32-bit elements; how exact they have to be, the bound alone decides.
A program may use at most 64 MiB of HBM per device.

v0:
```python
import math

import jax
import jax.numpy as jnp
from jax import lax
from jax.sharding import PartitionSpec as P

SWEEPS = 2
NS_STEPS = 20


def matmul(left, right):
    return jnp.dot(left, right, precision=lax.Precision.HIGHEST)


def polar_factor(gradient, count_steps):
    iterate = gradient / jnp.sqrt(jnp.sum(gradient * gradient))
    for count in range(count_steps):
        iterate = 1.5 * iterate - 0.5 * matmul(iterate, matmul(iterate.T, iterate))
    return iterate


def latitude_weight(rows, lat_total):
    degrees = -90.0 + (rows.astype(jnp.float32) + 0.5) * (180.0 / lat_total)
    return jnp.cos(degrees * (math.pi / 180.0))


def reduce_pair(cubic, colsq):
    return lax.psum((cubic, colsq), ("lat", "lon"))


def shards(loadings):
    lat_rows, lon_cols, modes = loadings.shape
    lat_total = lat_rows * lax.axis_size("lat")
    lon_total = lon_cols * lax.axis_size("lon")
    row_norm = jnp.sqrt(jnp.sum(loadings * loadings, axis=-1, keepdims=True) + 1e-06)
    normed = (loadings / row_norm).reshape(lat_rows * lon_cols, modes)
    own_rows = lax.axis_index("lat") * lat_rows + jnp.arange(lat_rows)
    weights = latitude_weight(own_rows, lat_total)
    weight_rows = jnp.repeat(weights, lon_cols).reshape(lat_rows * lon_cols, 1)
    total = jnp.sum(latitude_weight(jnp.arange(lat_total), lat_total)) * lon_total
    weighted = weight_rows * normed
    rotation = jnp.eye(modes, dtype=jnp.float32)
    gram = lax.psum(matmul(weighted.T, normed), ("lat", "lon"))
    for sweep_index in range(SWEEPS):
        spun = matmul(normed, rotation)
        cubic_local = matmul(weighted.T, spun * spun * spun)
        colsq_local = jnp.sum(weight_rows * spun * spun, axis=0)
        cubic, colsq = reduce_pair(cubic_local, colsq_local)
        gradient = cubic - matmul(gram, rotation) * (colsq / total)[None, :]
        rotation = polar_factor(gradient, NS_STEPS)
    rotated = matmul(normed, rotation).reshape(lat_rows, lon_cols, modes) * row_norm
    return (rotated, rotation)


def solution(mesh):
    return jax.shard_map(
        shards,
        mesh=mesh,
        in_specs=(P("lat", "lon", None),),
        out_specs=(P("lat", "lon", None), P()),
        check_vma=False,
    )
```

profile of v0, /device:TPU:0, one launch (start us, length us, event | category | flops | bytes accessed | tf_op | source)
XLA Modules:
  0.0 399.6 jit_solution(6151187368524490698)
XLA Ops:
  7.3 3.1 multiply_reduce_fusion
  10.6 2.3 broadcast_divide_fusion
  13.0 4.8 %reshape.28 = f32[3960,200]{1,0:T(8,128)} reshape(f32[22,180,200]{2,1,0:T(8,128)} %broadcast_divide_fusion) | data formatting | bytes 6336000 | tf_op jit(solution)/shard_map/reshape | solution.py:37
  17.8 11.0 %fusion.11 = f32[200,200]{1,0:T(8,128)} fusion(f32[22,180,200]{2,1,0:T(8,128)} %broadcast_divide_fusion, f32[22]{0:T(128)S(1)} %multiply_cosine_fusion), kind=kOutput, calls=%fused_computation.18 | convolution fusion | flops 1901592064 | bytes 3328088 | tf_op jit(solution)/shard_map/dot_general | solution.py:13
  29.0 3.9 copy.5
  32.9 4.8 %fusion.3 = (f32[200]{0:T(256)S(1)}, f32[3960,200]{0,1:T(8,128)S(1)}) fusion(f32[3960]{0:T(1024)S(1)} %mul.344, f32[3960,200]{1,0:T(8,128)} %reshape.28), kind=kOutput, calls=%fused_computation.8 | convolution fusion | flops 1903215872 | bytes 6352640 | tf_op jit(solution)/shard_map/dot_general | solution.py:13
  37.6 3.8 fusion.2
  41.5 0.6 cosine_reduce_fusion
  42.2 42.3 %psum.37 = f32[200]{0:T(256)S(1)} all-reduce(f32[200]{0:T(256)S(1)} %get-tuple-element.4), channel_id=1, replica_groups=mesh['lat'=8,'lon'=4] {'lat','lon'}, use_global_device_ids=true, to_apply=%region_4.0 | all-reduce | flops 200 | bytes 1600 | tf_op jit(solution)/shard_map/psum | solution.py:29
  85.0 87.1 %all-reduce.6.cloned.1.call-done = (f32[200,200]{1,0:T(8,128)}, f32[200,200]{1,0:T(8,128)}) async-done(((f32[200,200]{1,0:T(8,128)}, f32[200,200]{1,0:T(8,128)}), (f32[200,200]{1,0:T(8,128)}, f32[200,200]{1,0:T(8,128)})) %all-reduce.6.cloned.1.call-update) | async-done | bytes 320016 | tf_op jit(solution)/shard_map/psum | solution.py:29
  172.1 1.9 multiply_reduce_fusion.2
  174.7 0.5 fusion.58
  175.6 0.5 fusion.60
  176.5 0.5 fusion.61
  178.3 0.5 fusion.63
  179.1 0.5 fusion.64
  180.0 0.5 fusion.65
  180.9 0.5 fusion.66
  181.8 0.5 fusion.67
  182.7 0.5 fusion.68
  183.6 0.5 fusion.69
  184.4 0.5 fusion.70
  185.3 0.5 fusion.71
  186.2 0.5 fusion.72
  187.1 0.5 fusion.73
  188.0 0.7 fusion.74
  189.0 0.5 fusion.75
  190.8 0.5 fusion.77
  192.6 4.3 %fusion.5 = (f32[200]{0:T(256)S(1)}, f32[3960,200]{0,1:T(8,128)S(1)}) fusion(f32[3960]{0:T(1024)S(1)} %mul.344, f32[3960,200]{1,0:T(8,128)S(1)} %copy-done.1, f32[200,200]{1,0:T(8,128)S(1)} %fusion.35), kind=kOutput, calls=%fused_computation.10 | convolution fusion | flops 1903175808 | bytes 6512640 | tf_op jit(solution)/shard_map/dot_general | solution.py:13
  196.9 3.8 fusion.4
  200.7 41.3 %psum.39 = f32[200]{0:T(256)S(1)} all-reduce(f32[200]{0:T(256)S(1)} %get-tuple-element.8), channel_id=1, replica_groups=mesh['lat'=8,'lon'=4] {'lat','lon'}, use_global_device_ids=true, to_apply=%region_9.0 | all-reduce | flops 200 | bytes 1600 | tf_op jit(solution)/shard_map/psum | solution.py:29
  242.0 124.8 %all-reduce.4.cloned.1.call-done = f32[200,200]{1,0:T(8,128)} async-done(((f32[200,200]{1,0:T(8,128)}), f32[200,200]{1,0:T(8,128)}) %all-reduce.4.cloned.1.call-update) | async-done | bytes 160016 | tf_op jit(solution)/shard_map/psum | solution.py:29
  366.8 2.0 multiply_reduce_fusion.1
  369.4 0.5 fusion.59
  371.2 0.5 fusion.80
  373.0 0.5 fusion.82
  373.9 0.5 fusion.83
  374.7 0.5 fusion.84
  375.6 0.5 fusion.85
  376.5 0.5 fusion.86
  377.4 0.5 fusion.87
  378.3 0.5 fusion.88
  380.1 0.5 fusion.90
  381.8 0.5 fusion.92
  382.7 0.8 fusion.93
  383.9 0.5 fusion.94
  385.6 0.5 fusion.96
  387.4 4.9 %convolution_multiply_fusion = f32[22,180,200]{2,1,0:T(8,128)} fusion(f32[22,180,200]{2,1,0:T(8,128)S(1)} %copy-done, f32[22,180]{1,0:T(8,128)S(1)} %add_sqrt_fusion, f32[200,200]{1,0:T(8,128)S(1)} %fusion.14), kind=kOutput, calls=%fused_computation.13 | convolution fusion | flops 1901592064 | bytes 6511840 | tf_op jit(solution)/shard_map/dot_general | solution.py:13
  (67 shorter events, 18.6 us)
Async XLA Ops:
  7.2 165.0 %all-reduce.6.cloned.1.call-start = ((), (), s32[]{:S(2)}) async-start(), calls=%async_computation.1 | async-start | bytes 819200 | tf_op jit(solution)/shard_map/psum | solution.py:29
  7.2 3.4 copy-start.2
  41.5 325.3 %all-reduce.4.cloned.1.call-start = ((), (), s32[]{:S(2)}) async-start(), calls=%async_computation | async-start | bytes 409600 | tf_op jit(solution)/shard_map/psum | solution.py:29
  188.0 4.6 %copy-start.1 = (f32[3960,200]{1,0:T(8,128)S(1)}, f32[3960,200]{1,0:T(8,128)}, u32[]{:S(2)}) copy-start(f32[3960,200]{1,0:T(8,128)} %reshape.28) | copy-start | bytes 9504004
  382.7 4.7 %copy-start = (f32[22,180,200]{2,1,0:T(8,128)S(1)}, f32[22,180,200]{2,1,0:T(8,128)}, u32[]{:S(2)}) copy-start(f32[22,180,200]{2,1,0:T(8,128)} %broadcast_divide_fusion) | copy-start | bytes 9504004
  387.4 4.9 %copy-start.3 = (f32[200,200]{1,0:T(8,128)}, f32[200,200]{1,0:T(8,128)S(1)}, u32[]{:S(2)}) copy-start(f32[200,200]{1,0:T(8,128)S(1)} %fusion.14) | copy-start | bytes 480004
Sparse Core Ops, SparseCore 0:
  41.6 130.4 all-reduce.5
  242.1 124.6 all-reduce.3
where the time goes:
time: 407 us; the launch traced here: 400 us
  waiting for transfers between devices  212 us (52%)
  blocking collectives  83.5 us (21%)
  matrix products  71.6 us (18%)
  between operations  17.2 us (4%)
  local copies, waits for them, and re-layouts  9.12 us (2%)
  other arithmetic  6.21 us (2%)
    psum x2, waiting for transfers between devices, reduce_pair(): return lax.psum((cubic, colsq), ('lat', 'lon'))  212 us
    psum x2, blocking collectives, reduce_pair(): return lax.psum((cubic, colsq), ('lat', 'lon'))  83.5 us
    dot_general x88, matrix products, matmul(): return jnp.dot(left, right, precision=lax.Precision.HIGHEST)  71.6 us
    reshape x2, local copies, waits for them, and re-layouts, shards(): normed = (loadings / row_norm).reshape(lat_rows * lon_cols, modes)  8.73 us
  transfers between devices with their start and end apart: 2, of which 2 were waited for; matrix products, arithmetic and copies ran while one was open for 0% of the time, Pallas kernels for 0%

commit v1 on v0

v1 whole, which is shorter than its diff:
```python
import functools
import math

import jax
import jax.numpy as jnp
import numpy as np
from jax import lax
from jax.experimental import pallas as pl
from jax.experimental.pallas import tpu as pltpu
from jax.sharding import PartitionSpec as P

SWEEPS = 2
NS_STEPS = 20
SUB = 8
LANES = 256
MESH = pl.DeviceIdType.MESH
NN = (((1,), (0,)), ((), ()))
NT = (((1,), (1,)), ((), ()))


def split(value):
    high = value.astype(jnp.bfloat16)
    low = (value - high.astype(jnp.float32)).astype(jnp.bfloat16)
    return high, low


def mm(left, right, dims=NN):
    return lax.dot_general(left, right, dims, preferred_element_type=jnp.float32)


def mm3(left, right, dims=NN):
    lh, ll = left
    rh, rl = right
    return mm(lh, rh, dims) + (mm(lh, rl, dims) + mm(ll, rh, dims))


def polar(gradient):
    squares = jnp.sum(gradient * gradient, axis=0, keepdims=True)
    norm = jnp.sqrt(jnp.sum(squares, axis=1, keepdims=True))

    def step(_, x):
        parts = split(x)
        inner = mm3(parts, parts, NT)
        return 1.5 * x - 0.5 * mm3(split(inner), parts)

    return lax.fori_loop(0, NS_STEPS, step, gradient / norm)


class Reduce:
    def __init__(self, me, n, n_lon, owners, bufs, sems):
        self.me, self.n, self.n_lon, self.owners = me, n, n_lon, owners
        self.src, self.got, self.full = bufs
        self.sems = sems

    def copy(self, source, target, device, phase, sent, landed):
        return pltpu.make_async_remote_copy(
            src_ref=source,
            dst_ref=target,
            send_sem=self.sems.at[phase, sent],
            recv_sem=self.sems.at[phase + 1, landed],
            device_id=(device // self.n_lon, lax.rem(device, self.n_lon)),
            device_id_type=MESH,
        )

    def part(self, peer, source):
        return self.copy(self.src.at[peer], self.got.at[source], peer, 0, peer, source)

    def whole(self, peer, owner):
        return self.copy(self.full.at[owner], self.full.at[owner], peer, 2, peer, owner)

    def scatter(self):
        me, n = self.me, self.n
        for shift in range(1, n):
            peer = lax.rem(me + shift, n)

            @pl.when(peer < self.owners)
            def _():
                self.part(peer, me).start()

    def gather(self):
        me, n = self.me, self.n
        following = lax.rem(me + 1, n)

        @pl.when(me < self.owners)
        def _():
            acc = self.src[me]
            for shift in range(1, n):
                peer = lax.rem(me + n - shift, n)
                self.copy(self.src.at[me], self.got.at[peer], following, 0, peer, peer).wait_recv()
                acc = acc + self.got[peer]
            self.full[me] = acc
            for shift in range(1, n):
                self.whole(lax.rem(me + shift, n), me).start()

        for shift in range(1, n):
            peer = lax.rem(me + n - shift, n)

            @pl.when(peer < self.owners)
            def _():
                self.whole(following, peer).wait_recv()
                self.part(peer, me).wait_send()

        @pl.when(me < self.owners)
        def _():
            for shift in range(1, n):
                self.whole(lax.rem(me + shift, n), me).wait_send()


def kernel(n_lat, n_lon, total, weights, loadings, out, yh, yl, th, tl, gram, cubic,
           src1, got1, full1, src2, got2, full2, sems1, sems2):
    lat_rows, lon_cols, modes = loadings.shape
    n = n_lat * n_lon
    owners = modes // SUB
    lat, lon = lax.axis_index("lat"), lax.axis_index("lon")
    me = lat * n_lon + lon

    barrier = pltpu.get_barrier_semaphore()
    for shift in range(1, n):
        peer = lax.rem(me + shift, n)
        pl.semaphore_signal(barrier, inc=1, device_id=(peer // n_lon, lax.rem(peer, n_lon)),
                            device_id_type=MESH)

    gram[...] = jnp.zeros_like(gram)
    cubic[...] = jnp.zeros_like(cubic)

    def first(j, carry):
        weight = weights[0, lat * lat_rows + j]
        root = weights[1, lat * lat_rows + j]
        inverse = weights[2, lat * lat_rows + j]
        x = loadings[j]
        scale = root / jnp.sqrt(jnp.sum(x * x, axis=1, keepdims=True) + 1e-06)
        y = x * scale
        y_parts = split(y)
        t_parts = split(y.T)
        yh[j], yl[j] = y_parts
        th[j], tl[j] = t_parts
        gram[...] += mm3(t_parts, y_parts)
        cubic[...] += mm3(t_parts, split(y * y * y * inverse))
        return carry

    lax.fori_loop(0, lat_rows, first, 0)
    src1[:, 0, :, :modes] = gram[...].reshape(owners, SUB, modes)
    src1[:, 1, :, :modes] = cubic[...].reshape(owners, SUB, modes)

    pl.semaphore_wait(barrier, n - 1)
    reduce1 = Reduce(me, n, n_lon, owners, (src1, got1, full1), sems1)
    reduce1.scatter()
    reduce1.gather()
    whole = full1[:, 0, :, :modes].reshape(modes, modes)
    row = lax.broadcasted_iota(jnp.int32, (modes, modes), 0)
    col = lax.broadcasted_iota(jnp.int32, (modes, modes), 1)
    colsq = jnp.sum(jnp.where(row == col, whole, 0.0), axis=0, keepdims=True)
    gradient = full1[:, 1, :, :modes].reshape(modes, modes) - whole * (colsq / total)
    rotation = polar(gradient)

    r_parts = split(rotation)
    cubic[...] = jnp.zeros_like(cubic)

    def second(j, carry):
        inverse = weights[2, lat * lat_rows + j]
        spun = mm3((yh[j], yl[j]), r_parts)
        cubic[...] += mm3((th[j], tl[j]), split(spun * spun * spun * inverse))
        return carry

    lax.fori_loop(0, lat_rows, second, 0)
    src2[:, 0, :, :modes] = cubic[...].reshape(owners, SUB, modes)
    reduce2 = Reduce(me, n, n_lon, owners, (src2, got2, full2), sems2)
    reduce2.scatter()
    turned = mm3(split(whole), r_parts)
    colsq = jnp.sum(rotation * turned, axis=0, keepdims=True)
    reduce2.gather()
    gradient = full2[:, 0, :, :modes].reshape(modes, modes) - turned * (colsq / total)
    out[...] = polar(gradient)


def latitude_weight(lat_total):
    rows = np.arange(lat_total, dtype=np.float32)
    degrees = np.float32(-90.0) + (rows + np.float32(0.5)) * np.float32(180.0 / lat_total)
    return np.cos(degrees * np.float32(math.pi / 180.0)).astype(np.float32)


def shards(n_lat, n_lon, loadings):
    lat_rows, lon_cols, modes = loadings.shape
    n = n_lat * n_lon
    owners = modes // SUB
    assert modes % SUB == 0 and owners <= n and modes <= LANES
    weights = latitude_weight(lat_rows * n_lat)
    total = float(np.sum(weights, dtype=np.float32) * np.float32(lon_cols * n_lon))
    table = jnp.asarray(np.stack([weights, np.sqrt(weights), 1.0 / weights]).astype(np.float32))
    f32, bf16 = jnp.float32, jnp.bfloat16

    def bufs(parts):
        return [
            pltpu.VMEM((owners, parts, SUB, LANES), f32),
            pltpu.VMEM((n, parts, SUB, LANES), f32),
            pltpu.VMEM((owners, parts, SUB, LANES), f32),
        ]

    rotation = pl.pallas_call(
        functools.partial(kernel, n_lat, n_lon, total),
        out_shape=jax.ShapeDtypeStruct((modes, modes), f32),
        in_specs=[
            pl.BlockSpec(memory_space=pltpu.SMEM),
            pl.BlockSpec(memory_space=pltpu.VMEM),
        ],
        out_specs=pl.BlockSpec(memory_space=pltpu.VMEM),
        scratch_shapes=[
            pltpu.VMEM((lat_rows, lon_cols, modes), bf16),
            pltpu.VMEM((lat_rows, lon_cols, modes), bf16),
            pltpu.VMEM((lat_rows, modes, lon_cols), bf16),
            pltpu.VMEM((lat_rows, modes, lon_cols), bf16),
            pltpu.VMEM((modes, modes), f32),
            pltpu.VMEM((modes, modes), f32),
            *bufs(2),
            *bufs(1),
            pltpu.SemaphoreType.DMA((4, n)),
            pltpu.SemaphoreType.DMA((4, n)),
        ],
        compiler_params=pltpu.CompilerParams(
            collective_id=0, has_side_effects=True, vmem_limit_bytes=60 * 1024 * 1024
        ),
    )(table, loadings)
    rotated = jnp.einsum("abk,kl->abl", loadings, rotation, precision=lax.Precision.HIGH)
    return (rotated, rotation)


def solution(mesh):
    return jax.shard_map(
        functools.partial(shards, mesh.shape["lat"], mesh.shape["lon"]),
        mesh=mesh,
        in_specs=(P("lat", "lon", None),),
        out_specs=(P("lat", "lon", None), P()),
        check_vma=False,
    )
```

time: 407 us -> 103 us (0.25); the launches traced: 400 us -> 102 us
  waiting for transfers between devices: 212 us -> 0 us
  Pallas kernels: 0 us -> 94.9 us
  blocking collectives: 83.5 us -> 0 us
  matrix products: 71.6 us -> 6.14 us
  between operations: 17.2 us -> 0.65 us
  local copies, waits for them, and re-layouts: 9.12 us -> 0.68 us
  other arithmetic: 6.21 us -> 0 us
    psum x2 -> x0, waiting for transfers between devices: 212 us -> none  [reduce_pair(): return lax.psum((cubic, colsq), ('lat', 'lon'))]
    pallas_call x0 -> x1, Pallas kernels: none -> 94.9 us  [shards(): pl.pallas_call(functools.partial(kernel, n_lat, n_lon, total), out_shape=...]
    psum x2 -> x0, blocking collectives: 83.5 us -> none  [reduce_pair(): return lax.psum((cubic, colsq), ('lat', 'lon'))]
    dot_general x88 -> x1, matrix products: 71.6 us -> 6.14 us  [shards(): jnp.einsum('abk,kl->abl', loadings, rotation, precision=lax.Precision.HIGH)]
    reshape x2 -> x0, local copies, waits for them, and re-layouts: 8.73 us -> none  [shards(): normed = (loadings / row_norm).reshape(lat_rows * lon_cols, modes)]
  transfers between devices with their start and end apart: 2 -> 0, of which waited for: 2 -> 0; matrix products, arithmetic and copies ran while one was open for 0% -> 0% of each run, Pallas kernels for 0% -> 0%
where the time goes in v1:
time: 103 us; the launch traced here: 102 us
  Pallas kernels  94.9 us (92%)
  matrix products  6.14 us (6%)
    pallas_call x1, Pallas kernels, shards(): pl.pallas_call(functools.partial(kernel, n_lat, n_lon, total), out_shape=...  94.9 us
    dot_general x1, matrix products, shards(): jnp.einsum('abk,kl->abl', loadings, rotation, precision=lax.Precision.HIGH)  6.14 us

profile of v1, /device:TPU:0, one launch (start us, length us, event | category | flops | bytes accessed | tf_op | source)
XLA Modules:
  0.0 102.4 jit_solution(4322630305592581864)
XLA Ops:
  0.6 94.9 %shard_map.41 = f32[200,200]{1,0:T(8,128)} custom-call(f32[3,176]{1,0:T(4,128)} %constant.2.clone.weights, f32[22,180,200]{2,1,0:T(8,128)} %loadings.1), custom_call_target="tpu_custom_call" | custom-call | tf_op jit(solution)/shard_map/pallas_call | solution.py:199
  95.6 0.0 copy-start
  95.6 6.1 %convolution_bitcast_fusion = f32[22,180,200]{2,1,0:T(8,128)} fusion(f32[22,180,200]{2,1,0:T(8,128)} %loadings.1, f32[200,200]{1,0:T(8,128)} %shard_map.41), kind=kOutput, calls=%fused_computation | convolution fusion | flops 950400000 | bytes 6496000 | tf_op jit(solution)/shard_map/abk,kl->abl/dot_general | solution.py:223
  101.7 0.0 copy-done
  101.7 0.7 copy.5
Async XLA Ops:
  95.6 6.2 %copy-start = (f32[200,200]{1,0:T(8,128)S(1)}, f32[200,200]{1,0:T(8,128)}, u32[]{:S(2)}) copy-start(f32[200,200]{1,0:T(8,128)} %shard_map.41) | copy-start | bytes 480004

commit v2 on v1

--- a/solution.py
+++ b/solution.py
@@ -49,7 +49,7 @@
 class Reduce:
     def __init__(self, me, n, n_lon, owners, bufs, sems):
         self.me, self.n, self.n_lon, self.owners = me, n, n_lon, owners
-        self.src, self.got, self.full = bufs
+        self.src, self.got, self.full, self.rows = bufs
         self.sems = sems
 
     def copy(self, source, target, device, phase, sent, landed):
@@ -67,6 +67,27 @@
 
     def whole(self, peer, owner):
         return self.copy(self.full.at[owner], self.full.at[owner], peer, 2, peer, owner)
+
+    def row(self, peer, source):
+        return self.copy(self.rows.at[source], self.rows.at[source], peer, 4, peer, source)
+
+    def spread(self, value):
+        me, n = self.me, self.n
+        self.rows[me, :, : value.shape[1]] = value
+        for shift in range(1, n):
+            self.row(lax.rem(me + shift, n), me).start()
+
+    def total(self, width):
+        me, n = self.me, self.n
+        for shift in range(1, n):
+            peer = lax.rem(me + n - shift, n)
+            self.row(peer, peer).wait_recv()
+        acc = self.rows[0]
+        for source in range(1, n):
+            acc = acc + self.rows[source]
+        for shift in range(1, n):
+            self.row(lax.rem(me + shift, n), me).wait_send()
+        return acc[:, :width]
 
     def scatter(self):
         me, n = self.me, self.n
@@ -106,71 +127,101 @@
                 self.whole(lax.rem(me + shift, n), me).wait_send()
 
 
-def kernel(n_lat, n_lon, total, weights, loadings, out, yh, yl, th, tl, gram, cubic,
-           src1, got1, full1, src2, got2, full2, sems1, sems2):
-    lat_rows, lon_cols, modes = loadings.shape
+def kernel(n_lat, n_lon, total, weights, loadings, out, held, yh, yl, th, tl, gram, cubic,
+           src1, got1, full1, rows1, src2, got2, full2, rows2, sems1, sems2, loads):
+    lat_rows, lon_cols, modes = held.shape
     n = n_lat * n_lon
     owners = modes // SUB
+    unroll = 2 if lat_rows % 2 == 0 else 1
     lat, lon = lax.axis_index("lat"), lax.axis_index("lon")
     me = lat * n_lon + lon
-
+    reduce1 = Reduce(me, n, n_lon, owners, (src1, got1, full1, rows1), sems1)
+    reduce2 = Reduce(me, n, n_lon, owners, (src2, got2, full2, rows2), sems2)
+
+    def load(j):
+        return pltpu.make_async_copy(loadings.at[j], held.at[j], loads.at[j])
+
+    for j in range(lat_rows):
+        load(j).start()
     barrier = pltpu.get_barrier_semaphore()
     for shift in range(1, n):
         peer = lax.rem(me + shift, n)
         pl.semaphore_signal(barrier, inc=1, device_id=(peer // n_lon, lax.rem(peer, n_lon)),
                             device_id_type=MESH)
 
+    def rows_of(body, init):
+        def step(i, carry):
+            for k in range(unroll):
+                carry = body(i * unroll + k, carry)
+            return carry
+
+        return lax.fori_loop(0, lat_rows // unroll, step, init)
+
+    def normalise(j, colsq):
+        load(j).wait()
+        x = held[j]
+        root = weights[1, lat * lat_rows + j]
+        y = x * (root / jnp.sqrt(jnp.sum(x * x, axis=1, keepdims=True) + 1e-06))
+        held[j] = y
+        yh[j], yl[j] = split(y)
+        return colsq + jnp.sum(y * y, axis=0, keepdims=True)
+
+    none = jnp.zeros((1, modes), jnp.float32)
+    colsq = rows_of(normalise, none)
     gram[...] = jnp.zeros_like(gram)
     cubic[...] = jnp.zeros_like(cubic)
-
-    def first(j, carry):
-        weight = weights[0, lat * lat_rows + j]
-        root = weights[1, lat * lat_rows + j]
-        inverse = weights[2, lat * lat_rows + j]
-        x = loadings[j]
-        scale = root / jnp.sqrt(jnp.sum(x * x, axis=1, keepdims=True) + 1e-06)
-        y = x * scale
-        y_parts = split(y)
-        t_parts = split(y.T)
-        yh[j], yl[j] = y_parts
-        th[j], tl[j] = t_parts
-        gram[...] += mm3(t_parts, y_parts)
-        cubic[...] += mm3(t_parts, split(y * y * y * inverse))
+    pl.semaphore_wait(barrier, n - 1)
+    reduce1.spread(colsq)
+
+    def first(i, carry):
+        grams, cubics = [], []
+        for k in range(unroll):
+            j = i * unroll + k
+            y = held[j]
+            t_parts = split(y.T)
+            th[j], tl[j] = t_parts
+            inverse = weights[2, lat * lat_rows + j]
+            grams.append(mm3(t_parts, (yh[j], yl[j])))
+            cubics.append(mm3(t_parts, split(y * y * y * inverse)))
+        gram[...] += sum(grams[1:], grams[0])
+        cubic[...] += sum(cubics[1:], cubics[0])
         return carry
 
-    lax.fori_loop(0, lat_rows, first, 0)
-    src1[:, 0, :, :modes] = gram[...].reshape(owners, SUB, modes)
-    src1[:, 1, :, :modes] = cubic[...].reshape(owners, SUB, modes)
-
-    pl.semaphore_wait(barrier, n - 1)
-    reduce1 = Reduce(me, n, n_lon, owners, (src1, got1, full1), sems1)
+    lax.fori_loop(0, lat_rows // unroll, first, 0)
+    colsq = reduce1.total(modes)
+    local = cubic[...] - gram[...] * (colsq / total)
+    src1[:, :, :modes] = local.reshape(owners, SUB, modes)
     reduce1.scatter()
+    cubic[...] = jnp.zeros_like(cubic)
     reduce1.gather()
-    whole = full1[:, 0, :, :modes].reshape(modes, modes)
-    row = lax.broadcasted_iota(jnp.int32, (modes, modes), 0)
-    col = lax.broadcasted_iota(jnp.int32, (modes, modes), 1)
-    colsq = jnp.sum(jnp.where(row == col, whole, 0.0), axis=0, keepdims=True)
-    gradient = full1[:, 1, :, :modes].reshape(modes, modes) - whole * (colsq / total)
-    rotation = polar(gradient)
-
+    rotation = polar(full1[:, :, :modes].reshape(modes, modes))
     r_parts = split(rotation)
-    cubic[...] = jnp.zeros_like(cubic)
-
-    def second(j, carry):
-        inverse = weights[2, lat * lat_rows + j]
+
+    def spin(j, colsq):
         spun = mm3((yh[j], yl[j]), r_parts)
-        cubic[...] += mm3((th[j], tl[j]), split(spun * spun * spun * inverse))
+        held[j] = spun
+        return colsq + jnp.sum(spun * spun, axis=0, keepdims=True)
+
+    reduce2.spread(rows_of(spin, none))
+
+    def second(i, carry):
+        cubics = []
+        for k in range(unroll):
+            j = i * unroll + k
+            spun = held[j]
+            inverse = weights[2, lat * lat_rows + j]
+            cubics.append(mm3((th[j], tl[j]), split(spun * spun * spun * inverse)))
+        cubic[...] += sum(cubics[1:], cubics[0])
         return carry
 
-    lax.fori_loop(0, lat_rows, second, 0)
-    src2[:, 0, :, :modes] = cubic[...].reshape(owners, SUB, modes)
-    reduce2 = Reduce(me, n, n_lon, owners, (src2, got2, full2), sems2)
+    lax.fori_loop(0, lat_rows // unroll, second, 0)
+    turned = mm3(split(gram[...]), r_parts)
+    colsq = reduce2.total(modes)
+    local = cubic[...] - turned * (colsq / total)
+    src2[:, :, :modes] = local.reshape(owners, SUB, modes)
     reduce2.scatter()
-    turned = mm3(split(whole), r_parts)
-    colsq = jnp.sum(rotation * turned, axis=0, keepdims=True)
     reduce2.gather()
-    gradient = full2[:, 0, :, :modes].reshape(modes, modes) - turned * (colsq / total)
-    out[...] = polar(gradient)
+    out[...] = polar(full2[:, :, :modes].reshape(modes, modes))
 
 
 def latitude_weight(lat_total):
@@ -189,32 +240,34 @@
     table = jnp.asarray(np.stack([weights, np.sqrt(weights), 1.0 / weights]).astype(np.float32))
     f32, bf16 = jnp.float32, jnp.bfloat16
 
-    def bufs(parts):
-        return [
-            pltpu.VMEM((owners, parts, SUB, LANES), f32),
-            pltpu.VMEM((n, parts, SUB, LANES), f32),
-            pltpu.VMEM((owners, parts, SUB, LANES), f32),
-        ]
+    bufs = [
+        pltpu.VMEM((owners, SUB, LANES), f32),
+        pltpu.VMEM((n, SUB, LANES), f32),
+        pltpu.VMEM((owners, SUB, LANES), f32),
+        pltpu.VMEM((n, 1, LANES), f32),
+    ]
 
     rotation = pl.pallas_call(
         functools.partial(kernel, n_lat, n_lon, total),
         out_shape=jax.ShapeDtypeStruct((modes, modes), f32),
         in_specs=[
             pl.BlockSpec(memory_space=pltpu.SMEM),
-            pl.BlockSpec(memory_space=pltpu.VMEM),
+            pl.BlockSpec(memory_space=pl.ANY),
         ],
         out_specs=pl.BlockSpec(memory_space=pltpu.VMEM),
         scratch_shapes=[
+            pltpu.VMEM((lat_rows, lon_cols, modes), f32),
             pltpu.VMEM((lat_rows, lon_cols, modes), bf16),
             pltpu.VMEM((lat_rows, lon_cols, modes), bf16),
             pltpu.VMEM((lat_rows, modes, lon_cols), bf16),
             pltpu.VMEM((lat_rows, modes, lon_cols), bf16),
             pltpu.VMEM((modes, modes), f32),
             pltpu.VMEM((modes, modes), f32),
-            *bufs(2),
-            *bufs(1),
-            pltpu.SemaphoreType.DMA((4, n)),
-            pltpu.SemaphoreType.DMA((4, n)),
+            *bufs,
+            *bufs,
+            pltpu.SemaphoreType.DMA((6, n)),
+            pltpu.SemaphoreType.DMA((6, n)),
+            pltpu.SemaphoreType.DMA((lat_rows,)),
         ],
         compiler_params=pltpu.CompilerParams(
             collective_id=0, has_side_effects=True, vmem_limit_bytes=60 * 1024 * 1024

time: 103 us -> 88.5 us (0.86)
  Pallas kernels: 94.9 us -> 80.9 us
    pallas_call x1, Pallas kernels: 94.9 us -> 80.9 us  [shards(): pl.pallas_call(functools.partial(kernel, n_lat, n_lon, total), out_shape=...]
where the time goes in v2:
time: 88.5 us; the launch traced here: 88.3 us
  Pallas kernels  80.9 us (91%)
  matrix products  6.14 us (7%)
    pallas_call x1, Pallas kernels, shards(): pl.pallas_call(functools.partial(kernel, n_lat, n_lon, total), out_shape=...  80.9 us
    dot_general x1, matrix products, shards(): jnp.einsum('abk,kl->abl', loadings, rotation, precision=lax.Precision.HIGH)  6.14 us

profile of v2, /device:TPU:0, one launch (start us, length us, event | category | flops | bytes accessed | tf_op | source)
XLA Modules:
  0.0 88.3 jit_solution(1690004840284099149)
XLA Ops:
  0.6 80.9 %shard_map.41 = f32[200,200]{1,0:T(8,128)} custom-call(f32[3,176]{1,0:T(4,128)} %constant.2.clone.weights, f32[22,180,200]{2,1,0:T(8,128)} %loadings.1), custom_call_target="tpu_custom_call" | custom-call | tf_op jit(solution)/shard_map/pallas_call | solution.py:250
  81.5 0.0 copy-start
  81.5 6.1 %convolution_bitcast_fusion = f32[22,180,200]{2,1,0:T(8,128)} fusion(f32[22,180,200]{2,1,0:T(8,128)} %loadings.1, f32[200,200]{1,0:T(8,128)} %shard_map.41), kind=kOutput, calls=%fused_computation | convolution fusion | flops 950400000 | bytes 6496000 | tf_op jit(solution)/shard_map/abk,kl->abl/dot_general | solution.py:276
  87.6 0.0 copy-done
  87.7 0.7 copy.5
Async XLA Ops:
  81.5 6.2 %copy-start = (f32[200,200]{1,0:T(8,128)S(1)}, f32[200,200]{1,0:T(8,128)}, u32[]{:S(2)}) copy-start(f32[200,200]{1,0:T(8,128)} %shard_map.41) | copy-start | bytes 480004

commit v3 on v2

--- a/solution.py
+++ b/solution.py
@@ -43,7 +43,7 @@
         inner = mm3(parts, parts, NT)
         return 1.5 * x - 0.5 * mm3(split(inner), parts)
 
-    return lax.fori_loop(0, NS_STEPS, step, gradient / norm)
+    return lax.fori_loop(0, NS_STEPS, step, gradient / norm, unroll=4)
 
 
 class Reduce:
@@ -132,7 +132,7 @@
     lat_rows, lon_cols, modes = held.shape
     n = n_lat * n_lon
     owners = modes // SUB
-    unroll = 2 if lat_rows % 2 == 0 else 1
+    unroll = next(k for k in (11, 4, 3, 2, 1) if lat_rows % k == 0)
     lat, lon = lax.axis_index("lat"), lax.axis_index("lon")
     me = lat * n_lon + lon
     reduce1 = Reduce(me, n, n_lon, owners, (src1, got1, full1, rows1), sems1)

time: 88.5 us -> 83.4 us (0.942)
  Pallas kernels: 80.9 us -> 75.7 us
    pallas_call x1, Pallas kernels: 80.9 us -> 75.7 us  [shards(): pl.pallas_call(functools.partial(kernel, n_lat, n_lon, total), out_shape=...]
where the time goes in v3:
time: 83.4 us; the launch traced here: 83.2 us
  Pallas kernels  75.7 us (91%)
  matrix products  6.14 us (7%)
    pallas_call x1, Pallas kernels, shards(): pl.pallas_call(functools.partial(kernel, n_lat, n_lon, total), out_shape=...  75.7 us
    dot_general x1, matrix products, shards(): jnp.einsum('abk,kl->abl', loadings, rotation, precision=lax.Precision.HIGH)  6.14 us

profile of v3, /device:TPU:0, one launch (start us, length us, event | category | flops | bytes accessed | tf_op | source)
XLA Modules:
  0.0 83.2 jit_solution(3398472903786699602)
XLA Ops:
  0.6 75.7 %shard_map.41 = f32[200,200]{1,0:T(8,128)} custom-call(f32[3,176]{1,0:T(4,128)} %constant.2.clone.weights, f32[22,180,200]{2,1,0:T(8,128)} %loadings.1), custom_call_target="tpu_custom_call" | custom-call | tf_op jit(solution)/shard_map/pallas_call | solution.py:250
  76.4 0.0 copy-start
  76.4 6.1 %convolution_bitcast_fusion = f32[22,180,200]{2,1,0:T(8,128)} fusion(f32[22,180,200]{2,1,0:T(8,128)} %loadings.1, f32[200,200]{1,0:T(8,128)} %shard_map.41), kind=kOutput, calls=%fused_computation | convolution fusion | flops 950400000 | bytes 6496000 | tf_op jit(solution)/shard_map/abk,kl->abl/dot_general | solution.py:276
  82.5 0.0 copy-done
  82.5 0.7 copy.5
Async XLA Ops:
  76.4 6.2 %copy-start = (f32[200,200]{1,0:T(8,128)S(1)}, f32[200,200]{1,0:T(8,128)}, u32[]{:S(2)}) copy-start(f32[200,200]{1,0:T(8,128)} %shard_map.41) | copy-start | bytes 480004
